TPU v7x, 512 devices: a whole 4x4x16 slice. The times are simulated.
512 devices in a mesh: rows: 128 (over x, z_lo, y), cols: 4 (over z_hi, core).
Axes of the slice: x: 4, y: 4, z: 16 (z_hi: 2, z_lo: 8; z = z_hi * 8 + z_lo), core: 2. Of those that a mesh axis runs over, the one named last changes fastest.
Arguments:
- coords: int32 [8, 262144], P(None, ('rows', 'cols')), may hold values from 0 to 4095
- probes: float32 [64, 262144], P(None, ('rows', 'cols')), may hold values from -6 to 6
- lengthscales: float32 [8], replicated, may hold values from 0.15 to 0.25
- amplitude: float32 [1], replicated, may hold values from 0.1 to 0.3
- landmarks: float32 [254, 8, 128], replicated, may hold values from 0 to 1
- coupling: float32 [128, 128], replicated, may hold values from -0.5 to 0.5
Outputs:
- products: float32 [2, 64, 262144], P(None, None, ('rows', 'cols'))
All inputs are finite; a program needn't handle non-finite values.
Results may differ from a plain program's by a relative error of at most 0.0025.
Values may be sent and summed in bfloat16 or wider, within the bound.
No kernel may reach another device: no remote copies, remote signals or barrier semaphores. Data moves between devices by JAX's collectives and lax.ppermute only.
A program may use at most 64 MiB of HBM per device.

v0:
```python
import jax
import jax.numpy as jnp
from jax import lax
from jax.sharding import PartitionSpec as P


def over_pieces(array, axis):
    return lax.all_gather(array, axis).sum(0)


def swapped(array, axis, apart):
    return lax.ppermute(array, axis, [(i, i ^ 1 << apart) for i in range(lax.axis_size(axis))])


def pair_squares(left_points, right_points):
    squared = jnp.zeros((left_points.shape[1], right_points.shape[1]), jnp.float32)
    for component in range(left_points.shape[0]):
        offset = left_points[component][:, None] - right_points[component][None, :]
        squared = squared + offset * offset
    return squared


def on_device(coords, probes, lengthscales, amplitude, landmarks, coupling):
    highest = lax.Precision.HIGHEST
    inverse_scale = 1.0 / lengthscales
    scaled = coords.astype(jnp.float32) * (1.0 / 4096.0) * inverse_scale[:, None]
    strength = amplitude[0]
    signs_half = probes.astype(jnp.bfloat16)
    width = coords.shape[1]
    groups = lax.axis_size("cols")
    rows_index = lax.axis_index("rows")
    levels = lax.axis_size("rows").bit_length() - 1
    leaf_points = lax.all_gather(scaled, "cols", axis=1, tiled=True)
    leaf_signs = lax.all_gather(signs_half, "cols", axis=1, tiled=True)
    accumulated = jnp.zeros((2, probes.shape[0], width), jnp.float32)
    for row_block in range(groups):
        block_points = leaf_points[:, row_block * width : (row_block + 1) * width]
        block_signs = leaf_signs[:, row_block * width : (row_block + 1) * width]
        squared = pair_squares(block_points, scaled)
        kernel = strength * jnp.exp(-0.5 * squared)
        kernel_half = kernel.astype(jnp.bfloat16)
        slope_half = (kernel * squared).astype(jnp.bfloat16)
        accumulated = accumulated + jnp.stack(
            [
                jnp.dot(block_signs, kernel_half, preferred_element_type=jnp.float32),
                jnp.dot(block_signs, slope_half, preferred_element_type=jnp.float32),
            ]
        )
    result = accumulated
    factor_list = []
    dfactor_list = []
    for level in range(levels):
        depth = levels - level
        node = jnp.right_shift(rows_index, level)
        chosen = lax.dynamic_index_in_dim(landmarks, 2**depth - 2 + node, 0, keepdims=False)
        squared = pair_squares(scaled, chosen * inverse_scale[:, None])
        factor = strength * jnp.exp(-0.5 * squared)
        factor_list.append(factor)
        dfactor_list.append(factor * squared)
    factor_stack = jnp.stack(factor_list)
    dfactor_stack = jnp.stack(dfactor_list)
    own_project = jnp.einsum("pn,lnr->lpr", probes, factor_stack, precision=highest)
    own_dproject = jnp.einsum("pn,lnr->lpr", probes, dfactor_stack, precision=highest)
    projections = over_pieces(jnp.stack([own_project, own_dproject], axis=1), "cols")
    siblings = []
    pending = projections
    for level in range(levels):
        partner = swapped(pending[level:], "rows", level)
        siblings.append(partner[0])
        pending = pending.at[level + 1 :].add(partner[1:])
    for level in range(levels):
        sibling_sums = siblings[level]
        is_left = jnp.right_shift(rows_index, level) & 1 == 0
        core = jnp.where(is_left, coupling.T, coupling)
        first = jnp.dot(sibling_sums[0], core, precision=highest)
        second = jnp.dot(sibling_sums[1], core, precision=highest)
        value = jnp.dot(first, factor_stack[level].T, precision=highest)
        slope = jnp.dot(first, dfactor_stack[level].T, precision=highest) + jnp.dot(
            second, factor_stack[level].T, precision=highest
        )
        result = result + jnp.stack([value, slope])
    return result


def solution(mesh):
    in_specs = (P(None, ("rows", "cols")), P(None, ("rows", "cols")), P(), P(), P(), P())
    out_specs = P(None, None, ("rows", "cols"))
    return jax.shard_map(
        on_device, mesh=mesh, in_specs=in_specs, out_specs=out_specs, check_vma=False
    )
```

profile of v0, /device:TPU:8, one launch (start us, length us, event | category | flops | bytes accessed | tf_op | source)
XLA Modules:
  0.0 196.0 jit_solution(11825295575556073980)
XLA Ops:
  14.0 1.2 convolution_bitcast_fusion
  15.2 1.2 convolution_bitcast_fusion.1
  17.2 17.0 %all_gather.12 = f32[8,2048]{1,0:T(8,128)S(1)} all-gather(f32[8,512]{1,0:T(8,128)S(1)} %convert_multiply_fusion), channel_id=1, replica_groups=mesh['rows'=128,'cols'=4] {'cols'}, dimensions={1}, use_global_device_ids=true | all-gather | bytes 81920 | tf_op jit(solution)/shard_map/all_gather | solution.py:33
  34.3 18.0 %all_gather.13 = bf16[64,2048]{1,0:T(8,128)(2,1)S(1)} all-gather(bf16[64,512]{1,0:T(8,128)(2,1)S(1)} %convert_element_type.32), channel_id=1, replica_groups=mesh['rows'=128,'cols'=4] {'cols'}, dimensions={1}, use_global_device_ids=true | all-gather | bytes 327680 | tf_op jit(solution)/shard_map/all_gather | solution.py:34
  52.3 1.1 convolution_bitcast_fusion.3
  53.4 1.2 convolution_bitcast_fusion.2
  54.7 1.1 convolution_bitcast_fusion.5
  55.8 1.2 convolution_bitcast_fusion.4
  57.0 1.1 convolution_bitcast_fusion.7
  58.2 1.2 convolution_bitcast_fusion.6
  59.4 11.6 %all-gather.3.cloned.1.call-done = f32[28,2,64,128]{3,2,0,1:T(8,128)} async-done(((f32[7,2,64,128]{3,2,0,1:T(8,128)}), f32[28,2,64,128]{3,2,0,1:T(8,128)}) %all-gather.3.cloned.1.call-update) | async-done | bytes 1835024 | tf_op jit(solution)/shard_map/all_gather | solution.py:8
  71.1 1.7 reduce_sum.9
  72.7 3.6 %collective-permute-start = (f32[7,2,64,128]{3,2,0,1:T(8,128)S(1)}, f32[7,2,64,128]{3,2,0,1:T(8,128)S(1)}, u32[]{:S(2)}, u32[]{:S(2)}) collective-permute-start(f32[7,2,64,128]{3,2,0,1:T(8,128)S(1)} %reduce_sum.9), channel_id=1, source_target_pairs={{0,4},{4,0},{8,12},{12,8},{16,20},{20,16},{24,28},{28,24},{32,36},... | collective-permute-start | bytes 1376264 | tf_op jit(solution)/shard_map/ppermute | solution.py:12
  76.3 1.1 convolution_bitcast_fusion.9
  77.6 1.2 convolution_bitcast_fusion.8
  78.9 8.4 %collective-permute-done = f32[7,2,64,128]{3,2,0,1:T(8,128)S(1)} collective-permute-done((f32[7,2,64,128]{3,2,0,1:T(8,128)S(1)}, f32[7,2,64,128]{3,2,0,1:T(8,128)S(1)}, u32[]{:S(2)}, u32[]{:S(2)}) %collective-permute-start) | collective-permute-done | bytes 458784 | tf_op jit(solution)/shard_map/ppermute | solution.py:12
  87.3 4.4 %collective-permute-start.1 = (f32[6,2,64,128]{3,2,0,1:T(8,128)S(1)}, f32[6,2,64,128]{3,2,0,1:T(8,128)S(1)}, u32[]{:S(2)}, u32[]{:S(2)}) collective-permute-start(f32[6,2,64,128]{3,2,0,1:T(8,128)S(1)} %slice_add_fusion), channel_id=1, source_target_pairs={{0,8},{4,12},{8,0},{12,4},{16,24},{20,28},{24,16},{28,20},{32,40},... | collective-permute-start | bytes 1179656 | tf_op jit(solution)/shard_map/ppermute | solution.py:12
  94.1 1.0 fusion.6
  95.1 6.0 %collective-permute-done.1 = f32[6,2,64,128]{3,2,0,1:T(8,128)S(1)} collective-permute-done((f32[6,2,64,128]{3,2,0,1:T(8,128)S(1)}, f32[6,2,64,128]{3,2,0,1:T(8,128)S(1)}, u32[]{:S(2)}, u32[]{:S(2)}) %collective-permute-start.1) | collective-permute-done | bytes 393248 | tf_op jit(solution)/shard_map/ppermute | solution.py:12
  101.2 7.4 %collective-permute-start.2 = (f32[5,2,64,128]{3,2,0,1:T(8,128)S(1)}, f32[5,2,64,128]{3,2,0,1:T(8,128)S(1)}, u32[]{:S(2)}, u32[]{:S(2)}) collective-permute-start(f32[5,2,64,128]{3,2,0,1:T(8,128)S(1)} %slice_add_fusion.1), channel_id=1, source_target_pairs={{0,16},{4,20},{8,24},{12,28},{16,0},{20,4},{24,8},{28,12},{32,48},... | collective-permute-start | bytes 983048 | tf_op jit(solution)/shard_map/ppermute | solution.py:12
  109.0 1.0 fusion.50
  111.0 1.0 fusion.5
  112.0 3.0 %collective-permute-done.2 = f32[5,2,64,128]{3,2,0,1:T(8,128)S(1)} collective-permute-done((f32[5,2,64,128]{3,2,0,1:T(8,128)S(1)}, f32[5,2,64,128]{3,2,0,1:T(8,128)S(1)}, u32[]{:S(2)}, u32[]{:S(2)}) %collective-permute-start.2) | collective-permute-done | bytes 327712 | tf_op jit(solution)/shard_map/ppermute | solution.py:12
  115.0 7.8 %collective-permute-start.3 = (f32[4,2,64,128]{3,2,0,1:T(8,128)S(1)}, f32[4,2,64,128]{3,2,0,1:T(8,128)S(1)}, u32[]{:S(2)}, u32[]{:S(2)}) collective-permute-start(f32[4,2,64,128]{3,2,0,1:T(8,128)S(1)} %slice_add_fusion.2), channel_id=1, source_target_pairs={{0,32},{4,36},{8,40},{12,44},{16,48},{20,52},{24,56},{28,60},{32,0... | collective-permute-start | bytes 786440 | tf_op jit(solution)/shard_map/ppermute | solution.py:12
  126.2 6.7 %collective-permute-done.3 = f32[4,2,64,128]{3,2,0,1:T(8,128)S(1)} collective-permute-done((f32[4,2,64,128]{3,2,0,1:T(8,128)S(1)}, f32[4,2,64,128]{3,2,0,1:T(8,128)S(1)}, u32[]{:S(2)}, u32[]{:S(2)}) %collective-permute-start.3) | collective-permute-done | bytes 262176 | tf_op jit(solution)/shard_map/ppermute | solution.py:12
  132.8 21.1 %collective-permute-start.4 = (f32[3,2,64,128]{3,2,0,1:T(8,128)S(1)}, f32[3,2,64,128]{3,2,0,1:T(8,128)S(1)}, u32[]{:S(2)}, u32[]{:S(2)}) collective-permute-start(f32[3,2,64,128]{3,2,0,1:T(8,128)S(1)} %slice_add_fusion.3), channel_id=1, source_target_pairs={{0,64},{4,68},{8,72},{12,76},{16,80},{20,84},{24,88},{28,92},{32,9... | collective-permute-start | bytes 589832 | tf_op jit(solution)/shard_map/ppermute | solution.py:12
  154.2 1.0 fusion.46
  157.3 11.9 %collective-permute-done.4 = f32[3,2,64,128]{3,2,0,1:T(8,128)S(1)} collective-permute-done((f32[3,2,64,128]{3,2,0,1:T(8,128)S(1)}, f32[3,2,64,128]{3,2,0,1:T(8,128)S(1)}, u32[]{:S(2)}, u32[]{:S(2)}) %collective-permute-start.4) | collective-permute-done | bytes 196640 | tf_op jit(solution)/shard_map/ppermute | solution.py:12
  169.2 3.6 %collective-permute-start.5 = (f32[2,2,64,128]{3,2,0,1:T(8,128)S(1)}, f32[2,2,64,128]{3,2,0,1:T(8,128)S(1)}, u32[]{:S(2)}, u32[]{:S(2)}) collective-permute-start(f32[2,2,64,128]{3,2,0,1:T(8,128)S(1)} %slice_add_fusion.4), channel_id=1, source_target_pairs={{0,128},{4,132},{8,136},{12,140},{16,144},{20,148},{24,152},{28,15... | collective-permute-start | bytes 393224 | tf_op jit(solution)/shard_map/ppermute | solution.py:12
  176.6 4.9 %collective-permute-start.6 = (f32[1,2,64,128]{3,2,0,1:T(8,128)S(1)}, f32[1,2,64,128]{3,2,0,1:T(8,128)S(1)}, u32[]{:S(2)}, u32[]{:S(2)}) collective-permute-start(f32[1,2,64,128]{3,2,0,1:T(8,128)S(1)} %slice_add_fusion.5), channel_id=1, source_target_pairs={{0,256},{4,260},{8,264},{12,268},{16,272},{20,276},{24,280},{28,28... | collective-permute-start | bytes 196616 | tf_op jit(solution)/shard_map/ppermute | solution.py:12
  181.7 1.0 fusion.42
  188.2 1.0 fusion.39
  (64 shorter events, 26.6 us)
Async XLA Ops:
  6.5 64.5 %all-gather.3.cloned.1.call-start = ((), (), s32[]{:S(2)}) async-start(), calls=%async_computation | async-start | bytes 2293760 | tf_op jit(solution)/shard_map/all_gather | solution.py:8
  10.2 3.8 %copy-start.1 = (f32[64,512]{1,0:T(8,128)S(1)}, f32[64,512]{1,0:T(8,128)}, u32[]{:S(2)}) copy-start(f32[64,512]{1,0:T(8,128)} %param.19) | copy-start | bytes 393220
  72.7 14.5 %collective-permute-start = (f32[7,2,64,128]{3,2,0,1:T(8,128)S(1)}, f32[7,2,64,128]{3,2,0,1:T(8,128)S(1)}, u32[]{:S(2)}, u32[]{:S(2)}) collective-permute-start(f32[7,2,64,128]{3,2,0,1:T(8,128)S(1)} %reduce_sum.9), channel_id=1, source_target_pairs={{0,4},{4,0},{8,12},{12,8},{16,20},{20,16},{24,28},{28,24},{32,36},... | collective-permute-start | bytes 1376264 | tf_op jit(solution)/shard_map/ppermute | solution.py:12
  76.3 1.2 copy-start
  87.3 13.8 %collective-permute-start.1 = (f32[6,2,64,128]{3,2,0,1:T(8,128)S(1)}, f32[6,2,64,128]{3,2,0,1:T(8,128)S(1)}, u32[]{:S(2)}, u32[]{:S(2)}) collective-permute-start(f32[6,2,64,128]{3,2,0,1:T(8,128)S(1)} %slice_add_fusion), channel_id=1, source_target_pairs={{0,8},{4,12},{8,0},{12,4},{16,24},{20,28},{24,16},{28,20},{32,40},... | collective-permute-start | bytes 1179656 | tf_op jit(solution)/shard_map/ppermute | solution.py:12
  101.2 13.8 %collective-permute-start.2 = (f32[5,2,64,128]{3,2,0,1:T(8,128)S(1)}, f32[5,2,64,128]{3,2,0,1:T(8,128)S(1)}, u32[]{:S(2)}, u32[]{:S(2)}) collective-permute-start(f32[5,2,64,128]{3,2,0,1:T(8,128)S(1)} %slice_add_fusion.1), channel_id=1, source_target_pairs={{0,16},{4,20},{8,24},{12,28},{16,0},{20,4},{24,8},{28,12},{32,48},... | collective-permute-start | bytes 983048 | tf_op jit(solution)/shard_map/ppermute | solution.py:12
  115.0 17.8 %collective-permute-start.3 = (f32[4,2,64,128]{3,2,0,1:T(8,128)S(1)}, f32[4,2,64,128]{3,2,0,1:T(8,128)S(1)}, u32[]{:S(2)}, u32[]{:S(2)}) collective-permute-start(f32[4,2,64,128]{3,2,0,1:T(8,128)S(1)} %slice_add_fusion.2), channel_id=1, source_target_pairs={{0,32},{4,36},{8,40},{12,44},{16,48},{20,52},{24,56},{28,60},{32,0... | collective-permute-start | bytes 786440 | tf_op jit(solution)/shard_map/ppermute | solution.py:12
  132.8 36.4 %collective-permute-start.4 = (f32[3,2,64,128]{3,2,0,1:T(8,128)S(1)}, f32[3,2,64,128]{3,2,0,1:T(8,128)S(1)}, u32[]{:S(2)}, u32[]{:S(2)}) collective-permute-start(f32[3,2,64,128]{3,2,0,1:T(8,128)S(1)} %slice_add_fusion.3), channel_id=1, source_target_pairs={{0,64},{4,68},{8,72},{12,76},{16,80},{20,84},{24,88},{28,92},{32,9... | collective-permute-start | bytes 589832 | tf_op jit(solution)/shard_map/ppermute | solution.py:12
  169.2 7.3 %collective-permute-start.5 = (f32[2,2,64,128]{3,2,0,1:T(8,128)S(1)}, f32[2,2,64,128]{3,2,0,1:T(8,128)S(1)}, u32[]{:S(2)}, u32[]{:S(2)}) collective-permute-start(f32[2,2,64,128]{3,2,0,1:T(8,128)S(1)} %slice_add_fusion.4), channel_id=1, source_target_pairs={{0,128},{4,132},{8,136},{12,140},{16,144},{20,148},{24,152},{28,15... | collective-permute-start | bytes 393224 | tf_op jit(solution)/shard_map/ppermute | solution.py:12
  176.6 8.2 %collective-permute-start.6 = (f32[1,2,64,128]{3,2,0,1:T(8,128)S(1)}, f32[1,2,64,128]{3,2,0,1:T(8,128)S(1)}, u32[]{:S(2)}, u32[]{:S(2)}) collective-permute-start(f32[1,2,64,128]{3,2,0,1:T(8,128)S(1)} %slice_add_fusion.5), channel_id=1, source_target_pairs={{0,256},{4,260},{8,264},{12,268},{16,272},{20,276},{24,280},{28,28... | collective-permute-start | bytes 196616 | tf_op jit(solution)/shard_map/ppermute | solution.py:12
Sparse Core Ops, SparseCore 0:
  17.3 53.6 all-gather.2
where the time goes:
time: 197 us; the launch traced here: 196 us
  starting transfers between devices  52.9 us (27%)
  waiting for transfers between devices  48 us (24%)
  matrix products  35.1 us (18%)
  blocking collectives  35 us (18%)
  between operations  14.5 us (7%)
  other arithmetic  10.3 us (5%)
    ppermute x7, starting transfers between devices, swapped(): lax.ppermute(array, axis, [(i, i ^ 1 << apart) for i in range(lax.axis_si...  52.9 us
    ppermute x7, waiting for transfers between devices, swapped(): lax.ppermute(array, axis, [(i, i ^ 1 << apart) for i in range(lax.axis_si...  36.3 us
    all_gather x1, blocking collectives, on_device(): leaf_signs = lax.all_gather(signs_half, 'cols', axis=1, tiled=True)  18 us
    all_gather x1, blocking collectives, on_device(): leaf_points = lax.all_gather(scaled, 'cols', axis=1, tiled=True)  17 us
    all_gather x1, waiting for transfers between devices, over_pieces(): return lax.all_gather(array, axis).sum(0)  11.6 us
    dot_general x7, matrix products, on_device(): jnp.dot(first, dfactor_stack[level].T, precision=highest)  6.9 us
    dot_general x7, matrix products, on_device(): jnp.dot(second, factor_stack[level].T, precision=highest)  6.89 us
    dot_general x7, matrix products, on_device(): value = jnp.dot(first, factor_stack[level].T, precision=highest)  6.88 us
  transfers between devices with their start and end apart: 8, of which 7 were waited for; matrix products, arithmetic and copies ran while one was open for 15% of the time, Pallas kernels for 0%

commit v1 on v0

--- a/solution.py
+++ b/solution.py
@@ -30,8 +30,11 @@
     groups = lax.axis_size("cols")
     rows_index = lax.axis_index("rows")
     levels = lax.axis_size("rows").bit_length() - 1
-    leaf_points = lax.all_gather(scaled, "cols", axis=1, tiled=True)
-    leaf_signs = lax.all_gather(signs_half, "cols", axis=1, tiled=True)
+    leaf_points, leaf_signs = jnp.split(
+        lax.all_gather(jnp.concatenate([scaled, signs_half], axis=0), "cols", axis=1, tiled=True),
+        [scaled.shape[0]],
+        axis=0,
+    )
     accumulated = jnp.zeros((2, probes.shape[0], width), jnp.float32)
     for row_block in range(groups):
         block_points = leaf_points[:, row_block * width : (row_block + 1) * width]

time: 197 us -> 197 us (level)
  the two profiles are of different devices: /device:TPU:8 before, /device:TPU:24 now
where the time goes in v1:
time: 197 us
  waiting for transfers between devices  83.7 us (42%)
  matrix products  35.1 us (18%)
  starting transfers between devices  32.6 us (17%)
  blocking collectives  20.3 us (10%)
  between operations  14.5 us (7%)
  other arithmetic  10.4 us (5%)
    ppermute x7, waiting for transfers between devices, swapped(): lax.ppermute(array, axis, [(i, i ^ 1 << apart) for i in range(lax.axis_si...  45.7 us
    all_gather x1, waiting for transfers between devices, over_pieces(): return lax.all_gather(array, axis).sum(0)  38 us
    ppermute x7, starting transfers between devices, swapped(): lax.ppermute(array, axis, [(i, i ^ 1 << apart) for i in range(lax.axis_si...  32.6 us
    all_gather x1, blocking collectives, on_device(): lax.all_gather(jnp.concatenate([scaled, signs_half], axis=0), 'cols', axi...  20.3 us
    dot_general x7, matrix products, on_device(): jnp.dot(second, factor_stack[level].T, precision=highest)  6.89 us
    dot_general x7, matrix products, on_device(): jnp.dot(first, dfactor_stack[level].T, precision=highest)  6.89 us
    dot_general x7, matrix products, on_device(): value = jnp.dot(first, factor_stack[level].T, precision=highest)  6.88 us
    dot_general x4, matrix products, on_device(): jnp.dot(block_signs, slope_half, preferred_element_type=jnp.float32)  4.88 us
  transfers between devices with their start and end apart: 8, of which 7 were waited for; matrix products, arithmetic and copies ran while one was open for 15% of the time, Pallas kernels for 0%

profile of v1, /device:TPU:24, one launch (start us, length us, event | category | flops | bytes accessed | tf_op | source)
XLA Modules:
  0.0 196.8 jit_solution(9812842103140789349)
XLA Ops:
  14.0 1.2 convolution_bitcast_fusion
  15.2 1.2 convolution_bitcast_fusion.1
  17.3 20.3 %all_gather.9 = f32[72,2048]{1,0:T(8,128)S(1)} all-gather(f32[72,512]{1,0:T(8,128)S(1)} %pad_maximum_fusion.1), channel_id=1, replica_groups=mesh['rows'=128,'cols'=4] {'cols'}, dimensions={1}, use_global_device_ids=true | all-gather | bytes 737280 | tf_op jit(solution)/shard_map/all_gather | solution.py:34
  37.7 1.1 convolution_bitcast_fusion.3
  38.8 1.2 convolution_bitcast_fusion.2
  40.0 1.1 convolution_bitcast_fusion.5
  41.2 1.2 convolution_bitcast_fusion.4
  42.4 1.1 convolution_bitcast_fusion.7
  43.6 1.2 convolution_bitcast_fusion.6
  44.8 38.0 %all-gather.3.cloned.1.call-done = f32[28,2,64,128]{3,2,0,1:T(8,128)} async-done(((f32[7,2,64,128]{3,2,0,1:T(8,128)}), f32[28,2,64,128]{3,2,0,1:T(8,128)}) %all-gather.3.cloned.1.call-update) | async-done | bytes 1835024 | tf_op jit(solution)/shard_map/all_gather | solution.py:8
  82.8 1.7 reduce_sum.9
  84.4 2.7 %collective-permute-start = (f32[7,2,64,128]{3,2,0,1:T(8,128)S(1)}, f32[7,2,64,128]{3,2,0,1:T(8,128)S(1)}, u32[]{:S(2)}, u32[]{:S(2)}) collective-permute-start(f32[7,2,64,128]{3,2,0,1:T(8,128)S(1)} %reduce_sum.9), channel_id=1, source_target_pairs={{0,4},{4,0},{8,12},{12,8},{16,20},{20,16},{24,28},{28,24},{32,36},... | collective-permute-start | bytes 1376264 | tf_op jit(solution)/shard_map/ppermute | solution.py:12
  87.1 1.1 convolution_bitcast_fusion.9
  88.4 1.2 convolution_bitcast_fusion.8
  89.6 9.3 %collective-permute-done = f32[7,2,64,128]{3,2,0,1:T(8,128)S(1)} collective-permute-done((f32[7,2,64,128]{3,2,0,1:T(8,128)S(1)}, f32[7,2,64,128]{3,2,0,1:T(8,128)S(1)}, u32[]{:S(2)}, u32[]{:S(2)}) %collective-permute-start) | collective-permute-done | bytes 458784 | tf_op jit(solution)/shard_map/ppermute | solution.py:12
  99.0 2.2 %collective-permute-start.1 = (f32[6,2,64,128]{3,2,0,1:T(8,128)S(1)}, f32[6,2,64,128]{3,2,0,1:T(8,128)S(1)}, u32[]{:S(2)}, u32[]{:S(2)}) collective-permute-start(f32[6,2,64,128]{3,2,0,1:T(8,128)S(1)} %slice_add_fusion), channel_id=1, source_target_pairs={{0,8},{4,12},{8,0},{12,4},{16,24},{20,28},{24,16},{28,20},{32,40},... | collective-permute-start | bytes 1179656 | tf_op jit(solution)/shard_map/ppermute | solution.py:12
  103.6 1.0 fusion.6
  104.6 8.3 %collective-permute-done.1 = f32[6,2,64,128]{3,2,0,1:T(8,128)S(1)} collective-permute-done((f32[6,2,64,128]{3,2,0,1:T(8,128)S(1)}, f32[6,2,64,128]{3,2,0,1:T(8,128)S(1)}, u32[]{:S(2)}, u32[]{:S(2)}) %collective-permute-start.1) | collective-permute-done | bytes 393248 | tf_op jit(solution)/shard_map/ppermute | solution.py:12
  112.9 7.5 %collective-permute-start.2 = (f32[5,2,64,128]{3,2,0,1:T(8,128)S(1)}, f32[5,2,64,128]{3,2,0,1:T(8,128)S(1)}, u32[]{:S(2)}, u32[]{:S(2)}) collective-permute-start(f32[5,2,64,128]{3,2,0,1:T(8,128)S(1)} %slice_add_fusion.1), channel_id=1, source_target_pairs={{0,16},{4,20},{8,24},{12,28},{16,0},{20,4},{24,8},{28,12},{32,48},... | collective-permute-start | bytes 983048 | tf_op jit(solution)/shard_map/ppermute | solution.py:12
  122.7 1.0 fusion.5
  123.7 3.0 %collective-permute-done.2 = f32[5,2,64,128]{3,2,0,1:T(8,128)S(1)} collective-permute-done((f32[5,2,64,128]{3,2,0,1:T(8,128)S(1)}, f32[5,2,64,128]{3,2,0,1:T(8,128)S(1)}, u32[]{:S(2)}, u32[]{:S(2)}) %collective-permute-start.2) | collective-permute-done | bytes 327712 | tf_op jit(solution)/shard_map/ppermute | solution.py:12
  126.8 9.7 %collective-permute-start.3 = (f32[4,2,64,128]{3,2,0,1:T(8,128)S(1)}, f32[4,2,64,128]{3,2,0,1:T(8,128)S(1)}, u32[]{:S(2)}, u32[]{:S(2)}) collective-permute-start(f32[4,2,64,128]{3,2,0,1:T(8,128)S(1)} %slice_add_fusion.2), channel_id=1, source_target_pairs={{0,32},{4,36},{8,40},{12,44},{16,48},{20,52},{24,56},{28,60},{32,0... | collective-permute-start | bytes 786440 | tf_op jit(solution)/shard_map/ppermute | solution.py:12
  138.9 1.0 fusion.4
  139.9 6.4 %collective-permute-done.3 = f32[4,2,64,128]{3,2,0,1:T(8,128)S(1)} collective-permute-done((f32[4,2,64,128]{3,2,0,1:T(8,128)S(1)}, f32[4,2,64,128]{3,2,0,1:T(8,128)S(1)}, u32[]{:S(2)}, u32[]{:S(2)}) %collective-permute-start.3) | collective-permute-done | bytes 262176 | tf_op jit(solution)/shard_map/ppermute | solution.py:12
  146.3 1.9 collective-permute-start.4
  150.6 1.0 fusion.3
  151.6 18.4 %collective-permute-done.4 = f32[3,2,64,128]{3,2,0,1:T(8,128)S(1)} collective-permute-done((f32[3,2,64,128]{3,2,0,1:T(8,128)S(1)}, f32[3,2,64,128]{3,2,0,1:T(8,128)S(1)}, u32[]{:S(2)}, u32[]{:S(2)}) %collective-permute-start.4) | collective-permute-done | bytes 196640 | tf_op jit(solution)/shard_map/ppermute | solution.py:12
  169.9 3.7 %collective-permute-start.5 = (f32[2,2,64,128]{3,2,0,1:T(8,128)S(1)}, f32[2,2,64,128]{3,2,0,1:T(8,128)S(1)}, u32[]{:S(2)}, u32[]{:S(2)}) collective-permute-start(f32[2,2,64,128]{3,2,0,1:T(8,128)S(1)} %slice_add_fusion.4), channel_id=1, source_target_pairs={{0,128},{4,132},{8,136},{12,140},{16,144},{20,148},{24,152},{28,15... | collective-permute-start | bytes 393224 | tf_op jit(solution)/shard_map/ppermute | solution.py:12
  177.3 4.9 %collective-permute-start.6 = (f32[1,2,64,128]{3,2,0,1:T(8,128)S(1)}, f32[1,2,64,128]{3,2,0,1:T(8,128)S(1)}, u32[]{:S(2)}, u32[]{:S(2)}) collective-permute-start(f32[1,2,64,128]{3,2,0,1:T(8,128)S(1)} %slice_add_fusion.5), channel_id=1, source_target_pairs={{0,256},{4,260},{8,264},{12,268},{16,272},{20,276},{24,280},{28,28... | collective-permute-start | bytes 196616 | tf_op jit(solution)/shard_map/ppermute | solution.py:12
  182.4 1.0 fusion.42
  186.8 1.0 fusion.40
  188.9 1.0 fusion.39
  (64 shorter events, 25.6 us)
Async XLA Ops:
  6.5 76.2 %all-gather.3.cloned.1.call-start = ((), (), s32[]{:S(2)}) async-start(), calls=%async_computation | async-start | bytes 2293760 | tf_op jit(solution)/shard_map/all_gather | solution.py:8
  10.2 3.8 %copy-start.1 = (f32[64,512]{1,0:T(8,128)S(1)}, f32[64,512]{1,0:T(8,128)}, u32[]{:S(2)}) copy-start(f32[64,512]{1,0:T(8,128)} %param.19) | copy-start | bytes 393220
  84.4 14.5 %collective-permute-start = (f32[7,2,64,128]{3,2,0,1:T(8,128)S(1)}, f32[7,2,64,128]{3,2,0,1:T(8,128)S(1)}, u32[]{:S(2)}, u32[]{:S(2)}) collective-permute-start(f32[7,2,64,128]{3,2,0,1:T(8,128)S(1)} %reduce_sum.9), channel_id=1, source_target_pairs={{0,4},{4,0},{8,12},{12,8},{16,20},{20,16},{24,28},{28,24},{32,36},... | collective-permute-start | bytes 1376264 | tf_op jit(solution)/shard_map/ppermute | solution.py:12
  87.1 1.2 copy-start
  99.0 13.8 %collective-permute-start.1 = (f32[6,2,64,128]{3,2,0,1:T(8,128)S(1)}, f32[6,2,64,128]{3,2,0,1:T(8,128)S(1)}, u32[]{:S(2)}, u32[]{:S(2)}) collective-permute-start(f32[6,2,64,128]{3,2,0,1:T(8,128)S(1)} %slice_add_fusion), channel_id=1, source_target_pairs={{0,8},{4,12},{8,0},{12,4},{16,24},{20,28},{24,16},{28,20},{32,40},... | collective-permute-start | bytes 1179656 | tf_op jit(solution)/shard_map/ppermute | solution.py:12
  112.9 13.9 %collective-permute-start.2 = (f32[5,2,64,128]{3,2,0,1:T(8,128)S(1)}, f32[5,2,64,128]{3,2,0,1:T(8,128)S(1)}, u32[]{:S(2)}, u32[]{:S(2)}) collective-permute-start(f32[5,2,64,128]{3,2,0,1:T(8,128)S(1)} %slice_add_fusion.1), channel_id=1, source_target_pairs={{0,16},{4,20},{8,24},{12,28},{16,0},{20,4},{24,8},{28,12},{32,48},... | collective-permute-start | bytes 983048 | tf_op jit(solution)/shard_map/ppermute | solution.py:12
  126.8 19.5 %collective-permute-start.3 = (f32[4,2,64,128]{3,2,0,1:T(8,128)S(1)}, f32[4,2,64,128]{3,2,0,1:T(8,128)S(1)}, u32[]{:S(2)}, u32[]{:S(2)}) collective-permute-start(f32[4,2,64,128]{3,2,0,1:T(8,128)S(1)} %slice_add_fusion.2), channel_id=1, source_target_pairs={{0,32},{4,36},{8,40},{12,44},{16,48},{20,52},{24,56},{28,60},{32,0... | collective-permute-start | bytes 786440 | tf_op jit(solution)/shard_map/ppermute | solution.py:12
  146.3 23.6 %collective-permute-start.4 = (f32[3,2,64,128]{3,2,0,1:T(8,128)S(1)}, f32[3,2,64,128]{3,2,0,1:T(8,128)S(1)}, u32[]{:S(2)}, u32[]{:S(2)}) collective-permute-start(f32[3,2,64,128]{3,2,0,1:T(8,128)S(1)} %slice_add_fusion.3), channel_id=1, source_target_pairs={{0,64},{4,68},{8,72},{12,76},{16,80},{20,84},{24,88},{28,92},{32,9... | collective-permute-start | bytes 589832 | tf_op jit(solution)/shard_map/ppermute | solution.py:12
  169.9 7.3 %collective-permute-start.5 = (f32[2,2,64,128]{3,2,0,1:T(8,128)S(1)}, f32[2,2,64,128]{3,2,0,1:T(8,128)S(1)}, u32[]{:S(2)}, u32[]{:S(2)}) collective-permute-start(f32[2,2,64,128]{3,2,0,1:T(8,128)S(1)} %slice_add_fusion.4), channel_id=1, source_target_pairs={{0,128},{4,132},{8,136},{12,140},{16,144},{20,148},{24,152},{28,15... | collective-permute-start | bytes 393224 | tf_op jit(solution)/shard_map/ppermute | solution.py:12
  177.3 8.3 %collective-permute-start.6 = (f32[1,2,64,128]{3,2,0,1:T(8,128)S(1)}, f32[1,2,64,128]{3,2,0,1:T(8,128)S(1)}, u32[]{:S(2)}, u32[]{:S(2)}) collective-permute-start(f32[1,2,64,128]{3,2,0,1:T(8,128)S(1)} %slice_add_fusion.5), channel_id=1, source_target_pairs={{0,256},{4,260},{8,264},{12,268},{16,272},{20,276},{24,280},{28,28... | collective-permute-start | bytes 196616 | tf_op jit(solution)/shard_map/ppermute | solution.py:12
Sparse Core Ops, SparseCore 0:
  17.3 65.3 all-gather.2
